TPU v7x, 32 devices: a whole 2x2x4 slice. The times are simulated.
32 devices in a mesh: facet: 4 (over z), sub: 2 (over x), base: 4 (over y, core).
Axes of the slice: x: 2, y: 2, z: 4, core: 2. Of those that a mesh axis runs over, the one named last changes fastest.
Arguments:
- sky_image: bfloat16 [16384, 1024], P(('facet', 'base')), may hold values from -6 to 6
- facet_rows: int32 [4], replicated, may hold values from 0 to 126976
- column_offset: int32 [1], replicated, may hold values from 0 to 130816
- subgrid_offsets: int32 [2], replicated, may hold values from 0 to 130816
- vis_u: int32 [2, 32768], P('sub', ('facet', 'base')), may hold values from 0 to 1023
- vis_v: int32 [2, 32768], P('sub', ('facet', 'base')), may hold values from 0 to 1023
- observed: float32 [2, 2, 32768], P('sub', None, ('facet', 'base')), may hold values from -6 to 6
- weights: float32 [2, 32768], P('sub', ('facet', 'base')), may hold values from 0.3 to 3
- block_counts: int32 [2, 16], P('sub', ('facet', 'base')), may hold values from 1 to 16
Outputs:
- residual: float32 [2, 2, 32768], P('sub', None, ('facet', 'base'))
- facet_update: bfloat16 [16384, 1024], P(('facet', 'base'), 'sub')
Inputs may be any that keep to these rules, and one draw needn't show every extreme that they name: `block_counts`: the live blocks of a shard are its first ones.
All inputs are finite; a program needn't handle non-finite values.
Results may differ from a plain program's by a relative error of at most 0.008.
Values may be sent and summed in bfloat16 or wider, within the bound.
A program may use at most 64 MiB of HBM per device.

v0:
```python
import functools
import math

import jax
import jax.numpy as jnp
from jax import lax
from jax.experimental import pallas as pl
from jax.experimental.pallas import tpu as pltpu
from jax.sharding import PartitionSpec as P

NIMG = 131072
M = 256
SUBW = 1024
BLOCK = 128
MESH = pl.DeviceIdType.MESH
F32 = jnp.float32
BF16 = jnp.bfloat16


def unit(first, second, period):
    half = period // 2
    turn = ((first * second + half) & (period - 1)) - half
    y = turn.astype(F32) * (math.pi / period)
    q = y * y
    s = F32(-1.0 / 39916800.0)
    for k in (362880.0, -5040.0, 120.0, -6.0):
        s = s * q + F32(1.0 / k)
    s = (s * q + F32(1.0)) * y
    c = F32(1.0 / 479001600.0)
    for k in (-3628800.0, 40320.0, -720.0, 24.0, -2.0):
        c = c * q + F32(1.0 / k)
    c = c * q + F32(1.0)
    return F32(1.0) - F32(2.0) * s * s, F32(2.0) * s * c


def rows_iota(count, step=1):
    return lax.broadcasted_iota(jnp.int32, (count, 1), 0) * step


def lanes_iota(count):
    return lax.broadcasted_iota(jnp.int32, (1, count), 1)


def phase_product(coarse, fine, put):
    coarse_cos, coarse_sin = coarse
    fine_cos, fine_sin = fine
    for a in range(coarse_cos.shape[0]):
        ca, sa = coarse_cos[a : a + 1, :], coarse_sin[a : a + 1, :]
        put(a, ca * fine_cos - sa * fine_sin, sa * fine_cos + ca * fine_sin)


def pieces(groups, cols):
    row_blocks = min(groups, M // 16)
    col_blocks = groups // row_blocks
    height, width = M // row_blocks, cols // col_blocks
    return [
        (r * col_blocks + c, r * height, c * width, height, width)
        for r in range(row_blocks)
        for c in range(col_blocks)
    ]


def kernel(
    sizes,
    facet_rows,
    column_offset,
    subgrid_offsets,
    counts,
    sky_hbm,
    vis_u,
    vis_v,
    observed,
    weights,
    residual_out,
    share_out,
    t6,
    sky,
    t1,
    spec,
    t2,
    du,
    dv,
    t5,
    lhs,
    acc,
    zed,
    s_a,
    x_a,
    r_a,
    r_b,
    s_c,
    x_c,
    r_c,
    r_d,
    sky_sem,
    send_sem,
    recv_sem,
):
    n_facet, n_sub, n_base = sizes
    groups = n_facet * n_base
    total = groups * n_sub
    rows, columns = sky.shape
    vis = vis_u.shape[1]
    local_cols = t6.shape[1]
    facet, sub, base = lax.axis_index("facet"), lax.axis_index("sub"), lax.axis_index("base")
    me = facet * n_base + base
    everyone = sub * groups + me
    pairs = n_base // 2
    half_group, half_total = groups // 2, total // 2
    parity = lax.rem(base, 2)
    pair = facet * pairs + base // 2
    pair_all = sub * half_group + pair
    sibling = {"facet": facet, "sub": sub, "base": base + 1 - 2 * parity}

    def slot_of(g):
        f, b = g // n_base, g % n_base
        return (b % 2) * half_group + f * pairs + b // 2

    def like(index):
        inside = lax.rem(index, half_group)
        return {
            "facet": inside // pairs,
            "sub": index // half_group,
            "base": lax.rem(inside, pairs) * 2 + parity,
        }

    def member(index):
        return {"facet": index // n_base, "sub": sub, "base": lax.rem(index, n_base)}

    def anyone(index):
        inside = lax.rem(index, groups)
        return {
            "facet": inside // n_base,
            "sub": index // groups,
            "base": lax.rem(inside, n_base),
        }

    fetch = pltpu.make_async_copy(sky_hbm, sky, sky_sem)
    fetch.start()
    barrier = pltpu.get_barrier_semaphore()

    @pl.loop(1, total)
    def _(j):
        pl.semaphore_signal(
            barrier,
            inc=1,
            device_id=anyone(lax.rem(everyone + j, total)),
            device_id_type=MESH,
        )

    def wait_all(phase, buffer, count):
        whole = buffer.at[pl.ds(0, count)]
        done = pltpu.make_async_remote_copy(
            whole, whole, send_sem.at[phase], recv_sem.at[phase], member(me), MESH
        )
        done.wait_recv()
        done.wait_send()

    def scatter(phase, source, extra, landing):
        theirs = source.at[pl.ds((1 - parity) * half_group, half_group)]
        swap = pltpu.make_async_remote_copy(
            theirs, extra, send_sem.at[phase + 4], recv_sem.at[phase + 4], sibling, MESH
        )
        swap.start()
        swap.wait()
        for i in range(half_group):
            at = parity * half_group + i
            joint = source[at].astype(F32) + extra[i].astype(F32)
            source[at] = joint.astype(BF16)

        @pl.loop(1, half_group)
        def _(j):
            other = lax.rem(pair + j, half_group)
            pltpu.make_async_remote_copy(
                source.at[parity * half_group + other],
                landing.at[pair],
                send_sem.at[phase],
                recv_sem.at[phase],
                like(sub * half_group + other),
                MESH,
            ).start()

        landing[pair] = source[parity * half_group + pair]

    def gather(phase, buffer, slot, own, start, count):
        @pl.loop(1, count)
        def _(j):
            pltpu.make_async_remote_copy(
                buffer.at[slot],
                buffer.at[slot],
                send_sem.at[phase],
                recv_sem.at[phase],
                like(start + lax.rem(own + j, count)),
                MESH,
            ).start()

    def hand_over(phase, buffer, count):
        wait_all(phase, buffer, count - 1)
        mine = buffer.at[pl.ds(parity * count, count)]
        relay = pltpu.make_async_remote_copy(
            mine, mine, send_sem.at[phase + 4], recv_sem.at[phase + 4], sibling, MESH
        )
        relay.start()
        relay.wait()

    def summed(landing):
        result = landing[0].astype(F32)
        for g in range(1, half_group):
            result = result + landing[g].astype(F32)
        return result

    freq = column_offset[0] + lanes_iota(M)
    high = 128
    coarse = unit(rows_iota(columns // high, high), freq, NIMG)
    fine = unit(rows_iota(high), freq, NIMG)
    norm = F32(columns ** (-0.5))

    def put_t1(a, c, s):
        t1[a * high : (a + 1) * high, :M] = (c * norm).astype(BF16)
        t1[a * high : (a + 1) * high, M:] = (s * -norm).astype(BF16)

    phase_product(coarse, fine, put_t1)

    row_start = facet_rows[facet] + base * rows
    positions = row_start + lanes_iota(rows)
    own_offset = subgrid_offsets[sub]
    step = 32
    coarse = unit(own_offset + rows_iota(M // step, step), positions, NIMG)
    fine = unit(rows_iota(step), positions, NIMG)

    def put_t2(a, c, s):
        t2[a * step : (a + 1) * step, :rows] = c.astype(BF16)
        t2[a * step : (a + 1) * step, rows:] = s.astype(BF16)

    phase_product(coarse, fine, put_t2)
    fetch.wait()

    tile = min(256, rows)

    @pl.loop(0, rows // tile)
    def _(i):
        here = pl.ds(pl.multiple_of(i * tile, tile), tile)
        there = pl.ds(pl.multiple_of(rows + i * tile, tile), tile)
        part = jnp.dot(sky[here, :], t1[...], preferred_element_type=F32)
        real, imag = part[:, :M].astype(BF16), part[:, M:].astype(BF16)
        spec[here, :M] = real
        spec[here, M:] = imag
        spec[there, :M] = imag
        spec[there, M:] = -real

    def split(source, target, scale):
        blocks = pieces(groups, 2 * M)
        for g, r, c, height, width in blocks:
            target[slot_of(g)] = (source[r : r + height, c : c + width] * scale).astype(BF16)

    acc[:M, :] = jnp.dot(t2[...], spec[...], preferred_element_type=F32)
    split(acc, s_a, F32((rows * groups) ** (-0.5)))

    pl.semaphore_wait(barrier, total - 1)
    scatter(0, s_a, x_a, r_a)

    fan = 16

    def grid_table(position, table):
        width = 512
        for at in range(0, vis, width):
            lanes = slice(at, at + width)
            place = position[0:1, lanes]
            coarse = unit(rows_iota(M // fan, fan), place, SUBW)
            fine = unit(rows_iota(fan), place, SUBW)

            def put(a, c, s):
                table[a * fan : (a + 1) * fan, lanes] = c.astype(BF16)
                table[M + a * fan : M + (a + 1) * fan, lanes] = s.astype(BF16)

            phase_product(coarse, fine, put)

    grid_table(vis_u, du)
    wait_all(0, r_a, half_group - 1)
    slot = parity * half_group + pair
    r_b[slot] = summed(r_a).astype(BF16)
    gather(1, r_b, slot, pair, sub * half_group, half_group)
    grid_table(vis_v, dv)
    hand_over(1, r_b, half_group)

    for g, r, c, height, width in pieces(groups, 2 * M):
        block = r_b[slot_of(g)]
        part = min(width, M)
        for inner in range(0, width, part):
            value = block[:, inner : inner + part]
            at = c + inner
            lhs[r : r + height, at : at + part] = value
            if at < M:
                lhs[M + r : M + r + height, M + at : M + at + part] = -value
            else:
                lhs[M + r : M + r + height, at - M : at - M + part] = value

    chunk = 512
    acc[...] = jnp.zeros_like(acc)
    live = counts[0, 0] * BLOCK

    @pl.loop(0, vis // chunk)
    def _(i):
        lanes = pl.ds(pl.multiple_of(i * chunk, chunk), chunk)
        half = jnp.dot(lhs[...], du[:, lanes], preferred_element_type=F32)
        half_re, half_im = half[:M], half[M:]
        cos_v, sin_v = dv[:M, lanes].astype(F32), dv[M:, lanes].astype(F32)
        model_re = jnp.sum(cos_v * half_re + sin_v * half_im, axis=0, keepdims=True)
        model_im = jnp.sum(cos_v * half_im - sin_v * half_re, axis=0, keepdims=True)
        alive = lanes_iota(chunk) + i * chunk < live
        weight = weights[0:1, lanes]
        inv = F32(1.0 / M)
        res_re = jnp.where(alive, weight * (observed[0, 0:1, lanes] - model_re * inv), F32(0.0))
        res_im = jnp.where(alive, weight * (observed[0, 1:2, lanes] - model_im * inv), F32(0.0))
        residual_out[0, 0:1, lanes] = res_re
        residual_out[0, 1:2, lanes] = res_im
        r0 = res_re.astype(BF16).astype(F32)
        r1 = res_im.astype(BF16).astype(F32)
        cos_u, sin_u = du[:M, lanes].astype(F32), du[M:, lanes].astype(F32)
        spread = jnp.concatenate(
            [(cos_u * r0 - sin_u * r1).astype(BF16), (sin_u * r0 + cos_u * r1).astype(BF16)],
            axis=0,
        )
        acc[...] += lax.dot_general(
            dv[:, lanes], spread, (((1,), (1,)), ((), ())), preferred_element_type=F32
        )

    acc[:M, :M] = acc[:M, :M] - acc[M:, M:]
    acc[:M, M:] = acc[:M, M:] + acc[M:, :M]
    split(acc, s_c, F32((vis * groups) ** (-0.5)))
    scatter(2, s_c, x_c, r_c)

    for s in range(n_sub):
        freqs = subgrid_offsets[s] + lanes_iota(M)
        coarse = unit(row_start + rows_iota(rows // high, high), freqs, NIMG)
        fine = unit(rows_iota(high), freqs, NIMG)

        def put_t5(a, c, sine, at=2 * M * s):
            t5[a * high : (a + 1) * high, at : at + M] = c.astype(BF16)
            t5[a * high : (a + 1) * high, at + M : at + 2 * M] = sine.astype(BF16)

        phase_product(coarse, fine, put_t5)

    wait_all(2, r_c, half_group - 1)
    slot_all = parity * half_total + pair_all
    r_d[slot_all] = summed(r_c).astype(BF16)
    gather(3, r_d, slot_all, pair_all, 0, half_total)

    out_cols = sub * local_cols + lanes_iota(local_cols)
    coarse = unit(column_offset[0] + rows_iota(M // step, step), out_cols, NIMG)
    fine = unit(rows_iota(step), out_cols, NIMG)
    out_norm = F32(M ** (-0.5))

    def put_t6(a, c, s):
        t6[a * step : (a + 1) * step, :] = (c * out_norm).astype(BF16)
        t6[M + a * step : M + (a + 1) * step, :] = (s * -out_norm).astype(BF16)

    phase_product(coarse, fine, put_t6)
    hand_over(3, r_d, half_total)

    for s in range(n_sub):
        top = 2 * M * s
        for g, r, c, height, width in pieces(groups, 2 * M):
            place = slot_of(g)
            block = r_d[(place // half_group) * half_total + s * half_group + place % half_group]
            part = min(width, M)
            for inner in range(0, width, part):
                value = block[:, inner : inner + part]
                at = c + inner
                zed[top + r : top + r + height, at : at + part] = value
                low = top + M + r
                if at < M:
                    zed[low : low + height, M + at : M + at + part] = value
                else:
                    zed[low : low + height, at - M : at - M + part] = -value

    scale = F32((n_sub * M) ** (-0.5))

    @pl.loop(0, rows // tile)
    def _(i):
        here = pl.ds(pl.multiple_of(i * tile, tile), tile)
        part = jnp.dot(t5[here, :], zed[...], preferred_element_type=F32)
        share = (part * scale).astype(BF16)
        share_out[here, :] = share


def shards(
    sizes,
    sky_image,
    facet_rows,
    column_offset,
    subgrid_offsets,
    vis_u,
    vis_v,
    observed,
    weights,
    block_counts,
):
    n_facet, n_sub, n_base = sizes
    groups = n_facet * n_base
    rows, columns = sky_image.shape
    vis = vis_u.shape[1]
    local_cols = columns // n_sub
    _, _, _, height, width = pieces(groups, 2 * M)[0]
    smem = pl.BlockSpec(memory_space=pltpu.SMEM)
    vmem = pl.BlockSpec(memory_space=pltpu.VMEM)
    block = (groups, height, width)
    half_block = (groups // 2, height, width)
    residual, share, table = pl.pallas_call(
        functools.partial(kernel, sizes),
        out_shape=(
            jax.ShapeDtypeStruct(observed.shape, F32),
            jax.ShapeDtypeStruct((rows, 2 * M), BF16),
            jax.ShapeDtypeStruct((2 * M, local_cols), BF16),
        ),
        in_specs=[smem] * 4 + [pl.BlockSpec(memory_space=pl.ANY)] + [vmem] * 4,
        out_specs=(vmem, vmem, vmem),
        scratch_shapes=[
            pltpu.VMEM((rows, columns), BF16),
            pltpu.VMEM((columns, 2 * M), BF16),
            pltpu.VMEM((2 * rows, 2 * M), BF16),
            pltpu.VMEM((M, 2 * rows), BF16),
            pltpu.VMEM((2 * M, vis), BF16),
            pltpu.VMEM((2 * M, vis), BF16),
            pltpu.VMEM((rows, 2 * M * n_sub), BF16),
            pltpu.VMEM((2 * M, 2 * M), BF16),
            pltpu.VMEM((2 * M, 2 * M), F32),
            pltpu.VMEM((2 * M * n_sub, 2 * M), BF16),
            pltpu.VMEM(block, BF16),
            pltpu.VMEM(half_block, BF16),
            pltpu.VMEM(half_block, BF16),
            pltpu.VMEM(block, BF16),
            pltpu.VMEM(block, BF16),
            pltpu.VMEM(half_block, BF16),
            pltpu.VMEM(half_block, BF16),
            pltpu.VMEM((n_sub * groups, height, width), BF16),
            pltpu.SemaphoreType.DMA,
            pltpu.SemaphoreType.DMA((8,)),
            pltpu.SemaphoreType.DMA((8,)),
        ],
        compiler_params=pltpu.CompilerParams(
            collective_id=0, has_side_effects=True, vmem_limit_bytes=56 * 1024 * 1024
        ),
        name="column",
    )(
        facet_rows,
        column_offset,
        subgrid_offsets,
        block_counts,
        sky_image,
        vis_u,
        vis_v,
        observed,
        weights,
    )
    return residual, jnp.dot(share, table, preferred_element_type=F32).astype(BF16)


def solution(mesh):
    sizes = (mesh.shape["facet"], mesh.shape["sub"], mesh.shape["base"])
    return jax.shard_map(
        functools.partial(shards, sizes),
        mesh=mesh,
        in_specs=(
            P(("facet", "base"), None),
            P(),
            P(),
            P(),
            P("sub", ("facet", "base")),
            P("sub", ("facet", "base")),
            P("sub", None, ("facet", "base")),
            P("sub", ("facet", "base")),
            P("sub", ("facet", "base")),
        ),
        out_specs=(P("sub", None, ("facet", "base")), P(("facet", "base"), "sub")),
        check_vma=False,
    )
```

profile of v0, /device:TPU:0, one launch (start us, length us, event | category | flops | bytes accessed | tf_op | source)
XLA Modules:
  0.0 47.6 jit_solution(2159987750262701178)
XLA Ops:
  1.9 42.0 %column.1 = (f32[1,2,2048]{2,1,0:T(2,128)}, bf16[1024,512]{1,0:T(8,128)(2,1)}, bf16[512,512]{1,0:T(8,128)(2,1)}) custom-call(s32[4]{0:T(128)} %facet_rows.1, s32[1]{0:T(128)S(6)} %copy.12.column_offset, s32[2]{0:T(128)} %subgrid_offsets.1, s32[1,1]{1,0:T(1,128)S(6)} %copy.13.counts, bf16[1024,1024]{1,0:T(8,128)(2,1)} %sky_hbm.1, s32[1,2048]{1,0:T(1,128)} %vis_u.1, ...), custom_call_target="tpu_custom_call" | custom-call | tf_op jit(solution)/shard_map/column/pallas_call | solution.py:409
  43.9 0.0 copy-start
  43.9 3.0 %convolution_convert_fusion = bf16[1024,512]{1,0:T(8,128)(2,1)} fusion(bf16[1024,512]{1,0:T(8,128)(2,1)} %get-tuple-element.6, bf16[512,512]{1,0:T(8,128)(2,1)} %get-tuple-element.7), kind=kOutput, calls=%fused_computation | convolution fusion | flops 537395200 | bytes 2621440 | tf_op jit(solution)/shard_map/dot_general | solution.py:456
  46.9 0.0 copy-done
  46.9 0.6 %copy.14 = f32[1,2,2048]{2,1,0:T(2,128)} copy(f32[1,2,2048]{2,1,0:T(2,128)S(1)} %copy-done) | data formatting | bytes 32768
Async XLA Ops:
  43.9 3.0 %copy-start = (f32[1,2,2048]{2,1,0:T(2,128)S(1)}, f32[1,2,2048]{2,1,0:T(2,128)}, u32[]{:S(2)}) copy-start(f32[1,2,2048]{2,1,0:T(2,128)} %get-tuple-element.10) | copy-start | bytes 49156
where the time goes:
time: 47.8 us; the launch traced here: 47.6 us
  Pallas kernels  42 us (88%)
  matrix products  3.04 us (6%)
  between operations  1.94 us (4%)
  local copies, waits for them, and re-layouts  0.61 us (1%)
    pallas_call x1, Pallas kernels, shards(): pl.pallas_call(functools.partial(kernel, sizes), out_shape=(jax.ShapeDtyp...  42 us
    dot_general x1, matrix products, shards(): jnp.dot(share, table, preferred_element_type=F32).astype(BF16)  3.04 us

commit v1 on v0

v1 whole, which is shorter than its diff:
```python
import functools
import math

import jax
import jax.numpy as jnp
from jax import lax
from jax.experimental import pallas as pl
from jax.experimental.pallas import tpu as pltpu
from jax.sharding import PartitionSpec as P

NIMG = 131072
M = 256
SUBW = 1024
BLOCK = 128
MESH = pl.DeviceIdType.MESH
F32 = jnp.float32
BF16 = jnp.bfloat16


def unit(first, second, period):
    half = period // 2
    turn = ((first * second + half) & (period - 1)) - half
    y = turn.astype(F32) * (math.pi / period)
    q = y * y
    s = F32(-1.0 / 39916800.0)
    for k in (362880.0, -5040.0, 120.0, -6.0):
        s = s * q + F32(1.0 / k)
    s = (s * q + F32(1.0)) * y
    c = F32(1.0 / 479001600.0)
    for k in (-3628800.0, 40320.0, -720.0, 24.0, -2.0):
        c = c * q + F32(1.0 / k)
    c = c * q + F32(1.0)
    return F32(1.0) - F32(2.0) * s * s, F32(2.0) * s * c


def rows_iota(count, step=1):
    return lax.broadcasted_iota(jnp.int32, (count, 1), 0) * step


def lanes_iota(count):
    return lax.broadcasted_iota(jnp.int32, (1, count), 1)


def phase_product(coarse, fine, put):
    coarse_cos, coarse_sin = coarse
    fine_cos, fine_sin = fine
    for a in range(coarse_cos.shape[0]):
        ca, sa = coarse_cos[a : a + 1, :], coarse_sin[a : a + 1, :]
        put(a, ca * fine_cos - sa * fine_sin, sa * fine_cos + ca * fine_sin)


def pieces(groups, cols):
    row_blocks = min(groups, M // 16)
    col_blocks = groups // row_blocks
    height, width = M // row_blocks, cols // col_blocks
    return [
        (r * col_blocks + c, r * height, c * width, height, width)
        for r in range(row_blocks)
        for c in range(col_blocks)
    ]


def halves(groups):
    return 2 if groups <= M // 16 else 1


def far_first(count):
    return sorted(range(1, count), key=lambda j: (-min(j, count - j), j))


def kernel(
    sizes,
    facet_rows,
    column_offset,
    subgrid_offsets,
    counts,
    sky_hbm,
    vis_u_hbm,
    vis_v_hbm,
    observed_hbm,
    weights_hbm,
    residual_out,
    update,
    sky,
    vis_u,
    vis_v,
    observed,
    weights,
    t1,
    spec,
    t2,
    du,
    dv,
    t5,
    t6,
    lhs,
    acc,
    spread,
    zed,
    partial,
    share,
    s_a,
    x_a,
    r_a,
    r_b,
    s_c,
    x_c,
    r_c,
    r_d,
    sky_sem,
    side_sem,
    send_sem,
    recv_sem,
    d_send,
    d_recv,
):
    n_facet, n_sub, n_base = sizes
    groups = n_facet * n_base
    parts = halves(groups)
    wide = 2 * M // parts
    half = wide // 2
    rows, columns = sky.shape
    tile = min(256, rows)
    vis = vis_u.shape[1]
    local_cols = update.shape[1]
    facet, sub, base = lax.axis_index("facet"), lax.axis_index("sub"), lax.axis_index("base")
    pairs = n_base // 2
    half_group = groups // 2
    plane = n_sub * pairs
    parity = lax.rem(base, 2)
    row_of_base = base // 2
    pair = facet * pairs + row_of_base
    spot = sub * pairs + row_of_base
    sibling = {"facet": facet, "sub": sub, "base": base + 1 - 2 * parity}

    def slot_of(g):
        f, b = g // n_base, g % n_base
        return (b % 2) * half_group + f * pairs + b // 2

    def d_slot(which, f, place):
        return (which * n_facet + f) * plane + place

    def mate(j):
        other = lax.rem(pair + j, half_group)
        return other, {
            "facet": other // pairs,
            "sub": sub,
            "base": lax.rem(other, pairs) * 2 + parity,
        }

    def level(j):
        other = lax.rem(spot + j, plane)
        return {"facet": facet, "sub": other // pairs, "base": lax.rem(other, pairs) * 2 + parity}

    def above(j):
        return {"facet": lax.rem(facet + j, n_facet), "sub": sub, "base": base}

    def each(indices, body):
        if len(indices) <= 16:
            for j in indices:
                body(j)
        else:
            pl.loop(min(indices), max(indices) + 1)(body)

    fetches = []
    for i in range(rows // tile):
        here = pl.ds(i * tile, tile)
        fetches.append(
            pltpu.make_async_copy(sky_hbm.at[here, :], sky.at[here, :], sky_sem.at[i])
        )
        fetches[i].start()
    sides = [
        pltpu.make_async_copy(source, target, side_sem.at[i])
        for i, (source, target) in enumerate(
            (
                (vis_u_hbm, vis_u),
                (vis_v_hbm, vis_v),
                (observed_hbm, observed),
                (weights_hbm, weights),
            )
        )
    ]
    for side in sides:
        side.start()
    barrier = pltpu.get_barrier_semaphore()

    def greet(device):
        pl.semaphore_signal(barrier, inc=1, device_id=device, device_id_type=MESH)

    greet(sibling)
    each(range(1, half_group), lambda j: greet(mate(j)[1]))

    def greet_level(j):
        other = lax.rem(sub + 1 + j // pairs, n_sub)
        greet({"facet": facet, "sub": other, "base": lax.rem(j, pairs) * 2 + parity})

    each(range((n_sub - 1) * pairs), greet_level)
    partners = 1 + (half_group - 1) + (n_sub - 1) * pairs

    def wait_all(phase, c, buffer, count):
        whole = buffer.at[c, pl.ds(0, count)]
        done = pltpu.make_async_remote_copy(
            whole, whole, send_sem.at[phase, c], recv_sem.at[phase, c], sibling, MESH
        )
        done.wait_recv()
        done.wait_send()

    def swap(phase, c, source, extra):
        theirs = source.at[c, pl.ds((1 - parity) * half_group, half_group)]
        return pltpu.make_async_remote_copy(
            theirs,
            extra.at[c],
            send_sem.at[phase, c],
            recv_sem.at[phase, c],
            sibling,
            MESH,
        )

    def scatter(phase, c, source, extra, landing):
        for i in range(half_group):
            at = parity * half_group + i
            joint = source[c, at].astype(F32) + extra[c, i].astype(F32)
            source[c, at] = joint.astype(BF16)

        def send(j):
            other, device = mate(j)
            pltpu.make_async_remote_copy(
                source.at[c, parity * half_group + other],
                landing.at[c, pair],
                send_sem.at[phase, c],
                recv_sem.at[phase, c],
                device,
                MESH,
            ).start()

        each(far_first(half_group), send)
        landing[c, pair] = source[c, parity * half_group + pair]

    def summed(landing, c):
        result = landing[c, 0].astype(F32)
        for g in range(1, half_group):
            result = result + landing[c, g].astype(F32)
        return result.astype(BF16)

    def gather(phase, c, buffer):
        slot = parity * half_group + pair

        def send(j):
            pltpu.make_async_remote_copy(
                buffer.at[c, slot],
                buffer.at[c, slot],
                send_sem.at[phase, c],
                recv_sem.at[phase, c],
                mate(j)[1],
                MESH,
            ).start()

        each(far_first(half_group), send)

    def relay(phase, c, buffer):
        mine = buffer.at[c, pl.ds(parity * half_group, half_group)]
        return pltpu.make_async_remote_copy(
            mine, mine, send_sem.at[phase, c], recv_sem.at[phase, c], sibling, MESH
        )

    def split(c, target, scale):
        for g, r, k, height, width in pieces(groups, wide):
            target[c, slot_of(g)] = (acc[r : r + height, k : k + width] * scale).astype(BF16)

    high = 128
    step = 32
    freq = column_offset[0] + lanes_iota(M)
    coarse_1 = unit(rows_iota(columns // high, high), freq, NIMG)
    fine_1 = unit(rows_iota(high), freq, NIMG)
    norm = F32(columns ** (-0.5))

    def make_t1(c):
        lanes = slice(c * half, (c + 1) * half)

        def put(a, cosine, sine):
            t1[c, a * high : (a + 1) * high, :half] = (cosine * norm).astype(BF16)
            t1[c, a * high : (a + 1) * high, half:] = (sine * -norm).astype(BF16)

        phase_product([x[:, lanes] for x in coarse_1], [x[:, lanes] for x in fine_1], put)

    row_start = facet_rows[facet] + base * rows

    def make_spec(c):
        for i in range(rows // tile):
            here = slice(i * tile, (i + 1) * tile)
            there = slice(rows + i * tile, rows + (i + 1) * tile)
            if not c and not i % 2:
                for later in fetches[i : i + 2]:
                    later.wait()
            part = jnp.dot(sky[here, :], t1[c], preferred_element_type=F32)
            real, imag = part[:, :half].astype(BF16), part[:, half:].astype(BF16)
            spec[c, here, :half] = real
            spec[c, here, half:] = imag
            spec[c, there, :half] = imag
            spec[c, there, half:] = -real

    def contribution(c):
        for i in range(2):
            here = slice(i * M // 2, (i + 1) * M // 2)
            acc[here, :] = jnp.dot(t2[here, :], spec[c], preferred_element_type=F32)
        split(c, s_a, F32((rows * groups) ** (-0.5)))

    fan = 16

    def grid_table(position, table):
        width = 512
        for at in range(0, vis, width):
            lanes = slice(at, at + width)
            place = position[0:1, lanes]
            coarse = unit(rows_iota(M // fan, fan), place, SUBW)
            fine = unit(rows_iota(fan), place, SUBW)

            def put(a, c, s):
                table[a * fan : (a + 1) * fan, lanes] = c.astype(BF16)
                table[M + a * fan : M + (a + 1) * fan, lanes] = s.astype(BF16)

            phase_product(coarse, fine, put)

    make_t1(0)
    positions = row_start + lanes_iota(rows)
    own_offset = subgrid_offsets[sub]
    coarse_2 = unit(own_offset + rows_iota(M // step, step), positions, NIMG)
    fine_2 = unit(rows_iota(step), positions, NIMG)

    def put_t2(a, c, s):
        t2[a * step : (a + 1) * step, :rows] = c.astype(BF16)
        t2[a * step : (a + 1) * step, rows:] = s.astype(BF16)

    phase_product(coarse_2, fine_2, put_t2)
    swaps = []
    for c in range(parts):
        make_spec(c)
        if c:
            swaps[c - 1].wait()
            scatter(1, c - 1, s_a, x_a, r_a)
        contribution(c)
        if not c:
            pl.semaphore_wait(barrier, partners)
        swaps.append(swap(0, c, s_a, x_a))
        swaps[c].start()
        if c + 1 < parts:
            make_t1(c + 1)
    for side in sides:
        side.wait()
    grid_table(vis_u, du)
    swaps[-1].wait()
    scatter(1, parts - 1, s_a, x_a, r_a)
    grid_table(vis_v, dv)
    for c in range(parts):
        wait_all(1, c, r_a, half_group - 1)
        r_b[c, parity * half_group + pair] = summed(r_a, c)
        gather(2, c, r_b)

    for s in range(n_sub):
        freqs = subgrid_offsets[s] + lanes_iota(M)
        coarse = unit(row_start + rows_iota(rows // high, high), freqs, NIMG)
        fine = unit(rows_iota(high), freqs, NIMG)

        def put_t5(a, c, sine, at=2 * M * s):
            t5[a * high : (a + 1) * high, at : at + M] = c.astype(BF16)
            t5[a * high : (a + 1) * high, at + M : at + 2 * M] = sine.astype(BF16)

        phase_product(coarse, fine, put_t5)

    relays = []
    for c in range(parts):
        wait_all(2, c, r_b, half_group - 1)
        relays.append(relay(3, c, r_b))
        relays[c].start()

    for c in range(parts):
        relays[c].wait()
        for g, r, k, height, width in pieces(groups, wide):
            block = r_b[c, slot_of(g)]
            part = min(width, half)
            for inner in range(0, width, part):
                value = block[:, inner : inner + part]
                at = k + inner
                if at < half:
                    re = c * half + at
                    lhs[r : r + height, re : re + part] = value
                    lhs[M + r : M + r + height, M + re : M + re + part] = -value
                else:
                    im = c * half + at - half
                    lhs[r : r + height, M + im : M + im + part] = value
                    lhs[M + r : M + r + height, im : im + part] = value

    chunk = 512
    live = counts[0, 0] * BLOCK

    for i in range(vis // chunk):
        lanes = slice(i * chunk, (i + 1) * chunk)
        both = jnp.dot(lhs[...], du[:, lanes], preferred_element_type=F32)
        both_re, both_im = both[:M], both[M:]
        cos_v, sin_v = dv[:M, lanes].astype(F32), dv[M:, lanes].astype(F32)
        model_re = jnp.sum(cos_v * both_re + sin_v * both_im, axis=0, keepdims=True)
        model_im = jnp.sum(cos_v * both_im - sin_v * both_re, axis=0, keepdims=True)
        alive = lanes_iota(chunk) + i * chunk < live
        weight = weights[0:1, lanes]
        inv = F32(1.0 / M)
        res_re = jnp.where(alive, weight * (observed[0, 0:1, lanes] - model_re * inv), F32(0.0))
        res_im = jnp.where(alive, weight * (observed[0, 1:2, lanes] - model_im * inv), F32(0.0))
        residual_out[0, 0:1, lanes] = res_re
        residual_out[0, 1:2, lanes] = res_im

    across = (((1,), (1,)), ((), ()))
    swaps = []
    for c in range(parts):
        for i in range(vis // chunk):
            lanes = slice(i * chunk, (i + 1) * chunk)
            r0 = residual_out[0, 0:1, lanes].astype(BF16).astype(F32)
            r1 = residual_out[0, 1:2, lanes].astype(BF16).astype(F32)
            cos_u = du[c * half : (c + 1) * half, lanes].astype(F32)
            sin_u = du[M + c * half : M + (c + 1) * half, lanes].astype(F32)
            spread[c, :half, lanes] = (cos_u * r0 - sin_u * r1).astype(BF16)
            spread[c, half:, lanes] = (sin_u * r0 + cos_u * r1).astype(BF16)
        for i in range(2):
            here = slice(i * M, (i + 1) * M)
            acc[here, :] = lax.dot_general(
                dv[here, :], spread[c], across, preferred_element_type=F32
            )
        acc[:M, :half] = acc[:M, :half] - acc[M:, half:]
        acc[:M, half:] = acc[:M, half:] + acc[M:, :half]
        if c:
            swaps[c - 1].wait()
            scatter(5, c - 1, s_c, x_c, r_c)
        split(c, s_c, F32((vis * groups) ** (-0.5)))
        swaps.append(swap(4, c, s_c, x_c))
        swaps[c].start()

    out_cols = sub * local_cols + lanes_iota(local_cols)
    coarse = unit(column_offset[0] + rows_iota(M // step, step), out_cols, NIMG)
    fine = unit(rows_iota(step), out_cols, NIMG)
    out_norm = F32(M ** (-0.5))

    def put_t6(a, c, s):
        which, at = a * step // half, a * step % half
        t6[which, at : at + step, :] = (c * out_norm).astype(BF16)
        t6[which, half + at : half + at + step, :] = (s * -out_norm).astype(BF16)

    phase_product(coarse, fine, put_t6)
    swaps[-1].wait()
    scatter(5, parts - 1, s_c, x_c, r_c)

    def column_copy(c, j, slot, device):
        piece = r_d.at[c, slot]
        return pltpu.make_async_remote_copy(
            piece, piece, d_send.at[0, c, j], d_recv.at[0, c, j], device, MESH
        )

    def level_sends(c, j):
        slot = d_slot(parity, lax.rem(facet + n_facet - j, n_facet), spot)

        def send(q):
            pltpu.make_async_remote_copy(
                r_d.at[c, slot],
                r_d.at[c, slot],
                d_send.at[1, c, j],
                d_recv.at[1, c, j],
                level(q),
                MESH,
            ).start()

        each(far_first(plane), send)

    def level_done(c, j):
        slot = d_slot(parity, lax.rem(facet + n_facet - j, n_facet), 0)
        several = r_d.at[c, pl.ds(slot, plane - 1)]
        return pltpu.make_async_remote_copy(
            several, several, d_send.at[1, c, j], d_recv.at[1, c, j], sibling, MESH
        )

    def level_relay(c, j):
        slot = d_slot(parity, lax.rem(facet + n_facet - j, n_facet), 0)
        slab = r_d.at[c, pl.ds(slot, plane)]
        return pltpu.make_async_remote_copy(
            slab, slab, d_send.at[2, c, j], d_recv.at[2, c, j], sibling, MESH
        )

    nearest = far_first(n_facet)[::-1]
    own = d_slot(parity, facet, spot)
    for c in range(parts):
        wait_all(5, c, r_c, half_group - 1)
        r_d[c, own] = summed(r_c, c)
        for j in nearest[::-1]:
            column_copy(c, j, own, above(j)).start()
        level_sends(c, 0)
    for c in range(parts):
        for j in nearest:
            slot = d_slot(parity, lax.rem(facet + n_facet - j, n_facet), spot)
            column_copy(c, j, slot, above(j)).wait_recv()
            level_sends(c, j)
    for c in range(parts):
        for j in [0] + nearest:
            level_done(c, j).wait_recv()
            level_relay(c, j).start()

    scale = F32((n_sub * M) ** (-0.5))
    for c in range(parts):
        for j in [0] + nearest:
            level_relay(c, j).wait_recv()
        for s in range(n_sub):
            top = 2 * M * s
            for g, r, k, height, width in pieces(groups, wide):
                f, b = g // n_base, g % n_base
                block = r_d[c, d_slot(b % 2, f, s * pairs + b // 2)]
                part = min(width, half)
                low = top + M + r
                for inner in range(0, width, part):
                    value = block[:, inner : inner + part]
                    at = k + inner
                    zed[c, top + r : top + r + height, at : at + part] = value
                    if at < half:
                        zed[c, low : low + height, half + at : half + at + part] = value
                    else:
                        zed[c, low : low + height, at - half : at - half + part] = -value
        for i in range(rows // tile):
            here = slice(i * tile, (i + 1) * tile)
            wave = jnp.dot(t5[here, :], zed[c], preferred_element_type=F32)
            share[here, :] = (wave * scale).astype(BF16)
        for i in range(rows // tile):
            here = slice(i * tile, (i + 1) * tile)
            term = jnp.dot(share[here, :], t6[c], preferred_element_type=F32)
            if c:
                term = partial[here, :] + term
            if c + 1 < parts:
                partial[here, :] = term
            else:
                update[here, :] = term.astype(BF16)

    for c in range(parts):
        for j in [0] + nearest:
            level_done(c, j).wait_send()
            level_relay(c, j).wait_send()
            if j:
                column_copy(c, j, own, above(j)).wait_send()


def shards(
    sizes,
    sky_image,
    facet_rows,
    column_offset,
    subgrid_offsets,
    vis_u,
    vis_v,
    observed,
    weights,
    block_counts,
):
    n_facet, n_sub, n_base = sizes
    groups = n_facet * n_base
    parts = halves(groups)
    wide = 2 * M // parts
    rows, columns = sky_image.shape
    vis = vis_u.shape[1]
    local_cols = columns // n_sub
    _, _, _, height, width = pieces(groups, wide)[0]
    smem = pl.BlockSpec(memory_space=pltpu.SMEM)
    vmem = pl.BlockSpec(memory_space=pltpu.VMEM)
    hbm = pl.BlockSpec(memory_space=pltpu.HBM)
    block = (parts, groups, height, width)
    half_block = (parts, groups // 2, height, width)
    return pl.pallas_call(
        functools.partial(kernel, sizes),
        out_shape=(
            pltpu.VMEM(observed.shape, F32),
            pltpu.VMEM((rows, local_cols), BF16),
        ),
        in_specs=[smem] * 4 + [hbm] * 5,
        out_specs=(vmem, vmem),
        scratch_shapes=[
            pltpu.VMEM((rows, columns), BF16),
            pltpu.VMEM(vis_u.shape, jnp.int32),
            pltpu.VMEM(vis_v.shape, jnp.int32),
            pltpu.VMEM(observed.shape, F32),
            pltpu.VMEM(weights.shape, F32),
            pltpu.VMEM((parts, columns, wide), BF16),
            pltpu.VMEM((parts, 2 * rows, wide), BF16),
            pltpu.VMEM((M, 2 * rows), BF16),
            pltpu.VMEM((2 * M, vis), BF16),
            pltpu.VMEM((2 * M, vis), BF16),
            pltpu.VMEM((rows, 2 * M * n_sub), BF16),
            pltpu.VMEM((parts, wide, local_cols), BF16),
            pltpu.VMEM((2 * M, 2 * M), BF16),
            pltpu.VMEM((2 * M, wide), F32),
            pltpu.VMEM((parts, wide, vis), BF16),
            pltpu.VMEM((parts, 2 * M * n_sub, wide), BF16),
            pltpu.VMEM((rows, local_cols), F32),
            pltpu.VMEM((rows, wide), BF16),
            pltpu.VMEM(block, BF16),
            pltpu.VMEM(half_block, BF16),
            pltpu.VMEM(half_block, BF16),
            pltpu.VMEM(block, BF16),
            pltpu.VMEM(block, BF16),
            pltpu.VMEM(half_block, BF16),
            pltpu.VMEM(half_block, BF16),
            pltpu.VMEM((parts, n_sub * groups, height, width), BF16),
            pltpu.SemaphoreType.DMA((rows // min(256, rows),)),
            pltpu.SemaphoreType.DMA((4,)),
            pltpu.SemaphoreType.DMA((6, parts)),
            pltpu.SemaphoreType.DMA((6, parts)),
            pltpu.SemaphoreType.DMA((3, parts, n_facet)),
            pltpu.SemaphoreType.DMA((3, parts, n_facet)),
        ],
        compiler_params=pltpu.CompilerParams(
            collective_id=0, has_side_effects=True, vmem_limit_bytes=56 * 1024 * 1024
        ),
        name="column",
    )(
        facet_rows,
        column_offset,
        subgrid_offsets,
        block_counts,
        sky_image,
        vis_u,
        vis_v,
        observed,
        weights,
    )


def solution(mesh):
    sizes = (mesh.shape["facet"], mesh.shape["sub"], mesh.shape["base"])
    return jax.shard_map(
        functools.partial(shards, sizes),
        mesh=mesh,
        in_specs=(
            P(("facet", "base"), None),
            P(),
            P(),
            P(),
            P("sub", ("facet", "base")),
            P("sub", ("facet", "base")),
            P("sub", None, ("facet", "base")),
            P("sub", ("facet", "base")),
            P("sub", ("facet", "base")),
        ),
        out_specs=(P("sub", None, ("facet", "base")), P(("facet", "base"), "sub")),
        check_vma=False,
    )
```

time: 47.8 us -> 42.3 us (0.88)
  Pallas kernels: 42 us -> 38.6 us
  matrix products: 3.04 us -> 0 us
  local copies, waits for them, and re-layouts: 0.61 us -> 1.58 us
    pallas_call x1, Pallas kernels: 42 us -> 38.6 us  [shards(): pl.pallas_call(functools.partial(kernel, sizes), out_shape=(pltpu.VMEM(ob...]
    dot_general x1 -> x0, matrix products: 3.04 us -> none  [shards(): jnp.dot(share, table, preferred_element_type=F32).astype(BF16)]
    unnamed x3 -> x2, local copies, waits for them, and re-layouts: 0.61 us -> 1.58 us
where the time goes in v1:
time: 42.3 us; the launch traced here: 42.1 us
  Pallas kernels  38.6 us (91%)
  between operations  1.93 us (5%)
  local copies, waits for them, and re-layouts  1.58 us (4%)
    pallas_call x1, Pallas kernels, shards(): pl.pallas_call(functools.partial(kernel, sizes), out_shape=(pltpu.VMEM(ob...  38.6 us
    unnamed x2, local copies, waits for them, and re-layouts  1.58 us

profile of v1, /device:TPU:0, one launch (start us, length us, event | category | flops | bytes accessed | tf_op | source)
XLA Modules:
  0.0 42.1 jit_solution(11518021568106901381)
XLA Ops:
  1.9 38.6 %column.1 = (f32[1,2,2048]{2,1,0:T(2,128)S(1)}, bf16[1024,512]{1,0:T(8,128)(2,1)S(1)}) custom-call(s32[4]{0:T(128)} %facet_rows.1, s32[1]{0:T(128)S(6)} %copy.15.column_offset, s32[2]{0:T(128)} %subgrid_offsets.1, s32[1,1]{1,0:T(1,128)S(6)} %copy.16.counts, bf16[1024,1024]{1,0:T(8,128)(2,1)} %sky_hbm.1, s32[1,2048]{1,0:T(1,128)} %vis_u_hbm.1, ...), custom_call_target="tpu_custom_call" | custom-call | tf_op jit(solution)/shard_map/column/pallas_call | solution.py:569
  40.5 0.6 %copy.13 = f32[1,2,2048]{2,1,0:T(2,128)} copy(f32[1,2,2048]{2,1,0:T(2,128)S(1)} %get-tuple-element.2) | data formatting | bytes 32768
  41.2 1.0 %copy.14 = bf16[1024,512]{1,0:T(8,128)(2,1)} copy(bf16[1024,512]{1,0:T(8,128)(2,1)S(1)} %get-tuple-element.3) | data formatting | bytes 2097152

commit v2 on v1

--- a/solution.py
+++ b/solution.py
@@ -94,6 +94,7 @@
     t5,
     t6,
     lhs,
+    model,
     acc,
     spread,
     zed,
@@ -133,34 +134,28 @@
     spot = sub * pairs + row_of_base
     sibling = {"facet": facet, "sub": sub, "base": base + 1 - 2 * parity}
 
-    def slot_of(g):
-        f, b = g // n_base, g % n_base
-        return (b % 2) * half_group + f * pairs + b // 2
-
     def d_slot(which, f, place):
         return (which * n_facet + f) * plane + place
 
-    def mate(j):
-        other = lax.rem(pair + j, half_group)
-        return other, {
-            "facet": other // pairs,
-            "sub": sub,
-            "base": lax.rem(other, pairs) * 2 + parity,
-        }
-
-    def level(j):
-        other = lax.rem(spot + j, plane)
-        return {"facet": facet, "sub": other // pairs, "base": lax.rem(other, pairs) * 2 + parity}
-
-    def above(j):
-        return {"facet": lax.rem(facet + j, n_facet), "sub": sub, "base": base}
-
-    def each(indices, body):
-        if len(indices) <= 16:
-            for j in indices:
-                body(j)
-        else:
-            pl.loop(min(indices), max(indices) + 1)(body)
+    def by_distance(k):
+        edge = lax.min(facet, n_facet - 1 - facet)
+        across = facet + (k + 1) // 2 * (1 - k % 2 * 2)
+        beyond = jnp.where(2 * facet < n_facet, k, n_facet - 1 - k)
+        return jnp.where(k <= 2 * edge, across, beyond)
+
+    sources = [facet] + [by_distance(k) for k in range(1, n_facet)]
+    mates = [
+        (f * pairs + q, {"facet": f, "sub": sub, "base": q * 2 + parity})
+        for f in sources[:0:-1]
+        for q in [lax.rem(row_of_base + d, pairs) for d in range(pairs)]
+    ] + [
+        (facet * pairs + q, {"facet": facet, "sub": sub, "base": q * 2 + parity})
+        for q in [lax.rem(row_of_base + d, pairs) for d in range(1, pairs)]
+    ]
+    levels = [
+        {"facet": facet, "sub": other // pairs, "base": lax.rem(other, pairs) * 2 + parity}
+        for other in [lax.rem(spot + j, plane) for j in far_first(plane)]
+    ]
 
     fetches = []
     for i in range(rows // tile):
@@ -188,13 +183,11 @@
         pl.semaphore_signal(barrier, inc=1, device_id=device, device_id_type=MESH)
 
     greet(sibling)
-    each(range(1, half_group), lambda j: greet(mate(j)[1]))
-
-    def greet_level(j):
+    for _, device in mates:
+        greet(device)
+    for j in range((n_sub - 1) * pairs):
         other = lax.rem(sub + 1 + j // pairs, n_sub)
-        greet({"facet": facet, "sub": other, "base": lax.rem(j, pairs) * 2 + parity})
-
-    each(range((n_sub - 1) * pairs), greet_level)
+        greet({"facet": facet, "sub": other, "base": j % pairs * 2 + parity})
     partners = 1 + (half_group - 1) + (n_sub - 1) * pairs
 
     def wait_all(phase, c, buffer, count):
@@ -222,8 +215,7 @@
             joint = source[c, at].astype(F32) + extra[c, i].astype(F32)
             source[c, at] = joint.astype(BF16)
 
-        def send(j):
-            other, device = mate(j)
+        for other, device in mates:
             pltpu.make_async_remote_copy(
                 source.at[c, parity * half_group + other],
                 landing.at[c, pair],
@@ -232,8 +224,6 @@
                 device,
                 MESH,
             ).start()
-
-        each(far_first(half_group), send)
         landing[c, pair] = source[c, parity * half_group + pair]
 
     def summed(landing, c):
@@ -245,17 +235,15 @@
     def gather(phase, c, buffer):
         slot = parity * half_group + pair
 
-        def send(j):
+        for _, device in mates:
             pltpu.make_async_remote_copy(
                 buffer.at[c, slot],
                 buffer.at[c, slot],
                 send_sem.at[phase, c],
                 recv_sem.at[phase, c],
-                mate(j)[1],
+                device,
                 MESH,
             ).start()
-
-        each(far_first(half_group), send)
 
     def relay(phase, c, buffer):
         mine = buffer.at[c, pl.ds(parity * half_group, half_group)]
@@ -265,7 +253,7 @@
 
     def split(c, target, scale):
         for g, r, k, height, width in pieces(groups, wide):
-            target[c, slot_of(g)] = (acc[r : r + height, k : k + width] * scale).astype(BF16)
+            target[c, g] = (acc[r : r + height, k : k + width] * scale).astype(BF16)
 
     high = 128
     step = 32
@@ -373,33 +361,50 @@
         relays.append(relay(3, c, r_b))
         relays[c].start()
 
-    for c in range(parts):
-        relays[c].wait()
-        for g, r, k, height, width in pieces(groups, wide):
-            block = r_b[c, slot_of(g)]
+    top = M // 2
+
+    def make_lhs(which, c):
+        for g, r, k, height, width in pieces(groups, wide)[:half_group]:
+            block = r_b[c, which * half_group + g]
             part = min(width, half)
             for inner in range(0, width, part):
                 value = block[:, inner : inner + part]
                 at = k + inner
                 if at < half:
                     re = c * half + at
-                    lhs[r : r + height, re : re + part] = value
-                    lhs[M + r : M + r + height, M + re : M + re + part] = -value
+                    lhs[which, r : r + height, re : re + part] = value
+                    lhs[which, top + r : top + r + height, M + re : M + re + part] = -value
                 else:
                     im = c * half + at - half
-                    lhs[r : r + height, M + im : M + im + part] = value
-                    lhs[M + r : M + r + height, im : im + part] = value
+                    lhs[which, r : r + height, M + im : M + im + part] = value
+                    lhs[which, top + r : top + r + height, im : im + part] = value
 
     chunk = 512
     live = counts[0, 0] * BLOCK
 
+    def model_terms(which, lanes):
+        both = jnp.dot(lhs[which], du[:, lanes], preferred_element_type=F32)
+        both_re, both_im = both[:top], both[top:]
+        cos_v = dv[pl.ds(pl.multiple_of(which * top, top), top), lanes].astype(F32)
+        sin_v = dv[pl.ds(pl.multiple_of(M + which * top, top), top), lanes].astype(F32)
+        return (
+            jnp.sum(cos_v * both_re + sin_v * both_im, axis=0, keepdims=True),
+            jnp.sum(cos_v * both_im - sin_v * both_re, axis=0, keepdims=True),
+        )
+
+    for c in range(parts):
+        make_lhs(parity, c)
     for i in range(vis // chunk):
         lanes = slice(i * chunk, (i + 1) * chunk)
-        both = jnp.dot(lhs[...], du[:, lanes], preferred_element_type=F32)
-        both_re, both_im = both[:M], both[M:]
-        cos_v, sin_v = dv[:M, lanes].astype(F32), dv[M:, lanes].astype(F32)
-        model_re = jnp.sum(cos_v * both_re + sin_v * both_im, axis=0, keepdims=True)
-        model_im = jnp.sum(cos_v * both_im - sin_v * both_re, axis=0, keepdims=True)
+        model[0:1, lanes], model[1:2, lanes] = model_terms(parity, lanes)
+    for c in range(parts):
+        relays[c].wait()
+    for c in range(parts):
+        make_lhs(1 - parity, c)
+    for i in range(vis // chunk):
+        lanes = slice(i * chunk, (i + 1) * chunk)
+        model_re, model_im = model_terms(1 - parity, lanes)
+        model_re, model_im = model_re + model[0:1, lanes], model_im + model[1:2, lanes]
         alive = lanes_iota(chunk) + i * chunk < live
         weight = weights[0:1, lanes]
         inv = F32(1.0 / M)
@@ -413,12 +418,12 @@
     for c in range(parts):
         for i in range(vis // chunk):
             lanes = slice(i * chunk, (i + 1) * chunk)
-            r0 = residual_out[0, 0:1, lanes].astype(BF16).astype(F32)
-            r1 = residual_out[0, 1:2, lanes].astype(BF16).astype(F32)
-            cos_u = du[c * half : (c + 1) * half, lanes].astype(F32)
-            sin_u = du[M + c * half : M + (c + 1) * half, lanes].astype(F32)
-            spread[c, :half, lanes] = (cos_u * r0 - sin_u * r1).astype(BF16)
-            spread[c, half:, lanes] = (sin_u * r0 + cos_u * r1).astype(BF16)
+            r0 = residual_out[0, 0:1, lanes].astype(BF16)
+            r1 = residual_out[0, 1:2, lanes].astype(BF16)
+            cos_u = du[c * half : (c + 1) * half, lanes]
+            sin_u = du[M + c * half : M + (c + 1) * half, lanes]
+            spread[c, :half, lanes] = cos_u * r0 - sin_u * r1
+            spread[c, half:, lanes] = sin_u * r0 + cos_u * r1
         for i in range(2):
             here = slice(i * M, (i + 1) * M)
             acc[here, :] = lax.dot_general(
@@ -447,68 +452,58 @@
     swaps[-1].wait()
     scatter(5, parts - 1, s_c, x_c, r_c)
 
-    def column_copy(c, j, slot, device):
-        piece = r_d.at[c, slot]
+    def slab(c, f, count):
+        return r_d.at[c, pl.ds(d_slot(parity, f, 0), count)]
+
+    def column_copy(c, k, f, device, arrived):
+        piece = r_d.at[c, d_slot(parity, f, spot)]
         return pltpu.make_async_remote_copy(
-            piece, piece, d_send.at[0, c, j], d_recv.at[0, c, j], device, MESH
-        )
-
-    def level_sends(c, j):
-        slot = d_slot(parity, lax.rem(facet + n_facet - j, n_facet), spot)
-
-        def send(q):
-            pltpu.make_async_remote_copy(
-                r_d.at[c, slot],
-                r_d.at[c, slot],
-                d_send.at[1, c, j],
-                d_recv.at[1, c, j],
-                level(q),
-                MESH,
-            ).start()
-
-        each(far_first(plane), send)
-
-    def level_done(c, j):
-        slot = d_slot(parity, lax.rem(facet + n_facet - j, n_facet), 0)
-        several = r_d.at[c, pl.ds(slot, plane - 1)]
+            piece, piece, d_send.at[0, c, k], d_recv.at[0, c, arrived], device, MESH
+        )
+
+    def level_copy(c, f, piece, device):
         return pltpu.make_async_remote_copy(
-            several, several, d_send.at[1, c, j], d_recv.at[1, c, j], sibling, MESH
-        )
-
-    def level_relay(c, j):
-        slot = d_slot(parity, lax.rem(facet + n_facet - j, n_facet), 0)
-        slab = r_d.at[c, pl.ds(slot, plane)]
+            piece, piece, d_send.at[1, c, f], d_recv.at[1, c, f], device, MESH
+        )
+
+    def level_sends(c, f):
+        for device in levels:
+            level_copy(c, f, r_d.at[c, d_slot(parity, f, spot)], device).start()
+
+    def level_done(c, f):
+        return level_copy(c, f, slab(c, f, plane - 1), sibling)
+
+    def level_relay(c, f):
+        whole = slab(c, f, plane)
         return pltpu.make_async_remote_copy(
-            slab, slab, d_send.at[2, c, j], d_recv.at[2, c, j], sibling, MESH
-        )
-
-    nearest = far_first(n_facet)[::-1]
-    own = d_slot(parity, facet, spot)
+            whole, whole, d_send.at[2, c, f], d_recv.at[2, c, f], sibling, MESH
+        )
+
     for c in range(parts):
         wait_all(5, c, r_c, half_group - 1)
-        r_d[c, own] = summed(r_c, c)
-        for j in nearest[::-1]:
-            column_copy(c, j, own, above(j)).start()
-        level_sends(c, 0)
-    for c in range(parts):
-        for j in nearest:
-            slot = d_slot(parity, lax.rem(facet + n_facet - j, n_facet), spot)
-            column_copy(c, j, slot, above(j)).wait_recv()
-            level_sends(c, j)
-    for c in range(parts):
-        for j in [0] + nearest:
-            level_done(c, j).wait_recv()
-            level_relay(c, j).start()
+        r_d[c, d_slot(parity, facet, spot)] = summed(r_c, c)
+        for k in range(n_facet - 1, 0, -1):
+            device = {"facet": sources[k], "sub": sub, "base": base}
+            column_copy(c, k, facet, device, facet).start()
+        level_sends(c, facet)
+    for c in range(parts):
+        for k in range(1, n_facet):
+            column_copy(c, k, sources[k], sibling, sources[k]).wait_recv()
+            level_sends(c, sources[k])
+    for c in range(parts):
+        for f in sources:
+            level_done(c, f).wait_recv()
+            level_relay(c, f).start()
 
     scale = F32((n_sub * M) ** (-0.5))
     for c in range(parts):
-        for j in [0] + nearest:
-            level_relay(c, j).wait_recv()
+        for f in sources:
+            level_relay(c, f).wait_recv()
         for s in range(n_sub):
             top = 2 * M * s
             for g, r, k, height, width in pieces(groups, wide):
-                f, b = g // n_base, g % n_base
-                block = r_d[c, d_slot(b % 2, f, s * pairs + b // 2)]
+                which, place = g // half_group, g % half_group
+                block = r_d[c, d_slot(which, place // pairs, s * pairs + place % pairs)]
                 part = min(width, half)
                 low = top + M + r
                 for inner in range(0, width, part):
@@ -534,11 +529,22 @@
                 update[here, :] = term.astype(BF16)
 
     for c in range(parts):
-        for j in [0] + nearest:
-            level_done(c, j).wait_send()
-            level_relay(c, j).wait_send()
-            if j:
-                column_copy(c, j, own, above(j)).wait_send()
+        for k in range(n_facet):
+            level_done(c, sources[k]).wait_send()
+            level_relay(c, sources[k]).wait_send()
+            if k:
+                column_copy(c, k, facet, sibling, facet).wait_send()
+
+
+def deliver(residual, update, residual_out, update_out, sems):
+    copies = [
+        pltpu.make_async_copy(residual, residual_out, sems.at[0]),
+        pltpu.make_async_copy(update, update_out, sems.at[1]),
+    ]
+    for copy in copies:
+        copy.start()
+    for copy in copies:
+        copy.wait()
 
 
 def shards(
@@ -566,7 +572,7 @@
     hbm = pl.BlockSpec(memory_space=pltpu.HBM)
     block = (parts, groups, height, width)
     half_block = (parts, groups // 2, height, width)
-    return pl.pallas_call(
+    residual, update = pl.pallas_call(
         functools.partial(kernel, sizes),
         out_shape=(
             pltpu.VMEM(observed.shape, F32),
@@ -587,7 +593,8 @@
             pltpu.VMEM((2 * M, vis), BF16),
             pltpu.VMEM((rows, 2 * M * n_sub), BF16),
             pltpu.VMEM((parts, wide, local_cols), BF16),
-            pltpu.VMEM((2 * M, 2 * M), BF16),
+            pltpu.VMEM((2, M, 2 * M), BF16),
+            pltpu.VMEM((2, vis), F32),
             pltpu.VMEM((2 * M, wide), F32),
             pltpu.VMEM((parts, wide, vis), BF16),
             pltpu.VMEM((parts, 2 * M * n_sub, wide), BF16),
@@ -623,6 +630,20 @@
         observed,
         weights,
     )
+    return pl.pallas_call(
+        deliver,
+        out_shape=(
+            jax.ShapeDtypeStruct(residual.shape, F32),
+            jax.ShapeDtypeStruct(update.shape, BF16),
+        ),
+        in_specs=[vmem] * 2,
+        out_specs=(hbm, hbm),
+        scratch_shapes=[pltpu.SemaphoreType.DMA((2,))],
+        name="deliver",
+    )(
+        pltpu.with_memory_space_constraint(residual, pltpu.VMEM),
+        pltpu.with_memory_space_constraint(update, pltpu.VMEM),
+    )
 
 
 def solution(mesh):

time: 42.3 us -> 39.4 us (0.931)
  local copies, waits for them, and re-layouts: 1.58 us -> 0 us
  Pallas kernels: 38.6 us -> 37.3 us
    pallas_call x1, Pallas kernels: 38.6 us -> 36.3 us  [shards(): pl.pallas_call(functools.partial(kernel, sizes), out_shape=(pltpu.VMEM(ob...]
    unnamed x2 -> x0, local copies, waits for them, and re-layouts: 1.58 us -> none
    pallas_call x0 -> x1, Pallas kernels: none -> 1 us  [shards(): pl.pallas_call(deliver, out_shape=(jax.ShapeDtypeStruct(residual.shape, F...]
where the time goes in v2:
time: 39.4 us; the launch traced here: 39.2 us
  Pallas kernels  37.3 us (95%)
  between operations  1.93 us (5%)
    pallas_call x1, Pallas kernels, shards(): pl.pallas_call(functools.partial(kernel, sizes), out_shape=(pltpu.VMEM(ob...  36.3 us
    pallas_call x1, Pallas kernels, shards(): pl.pallas_call(deliver, out_shape=(jax.ShapeDtypeStruct(residual.shape, F...  1 us

profile of v2, /device:TPU:0, one launch (start us, length us, event | category | flops | bytes accessed | tf_op | source)
XLA Modules:
  0.0 39.2 jit_solution(9895020758355953654)
XLA Ops:
  1.9 36.3 %column.1 = (f32[1,2,2048]{2,1,0:T(2,128)S(1)}, bf16[1024,512]{1,0:T(8,128)(2,1)S(1)}) custom-call(s32[4]{0:T(128)} %facet_rows.1, s32[1]{0:T(128)S(6)} %copy.11.column_offset, s32[2]{0:T(128)} %subgrid_offsets.1, s32[1,1]{1,0:T(1,128)S(6)} %copy.12.counts, bf16[1024,1024]{1,0:T(8,128)(2,1)} %sky_hbm.1, s32[1,2048]{1,0:T(1,128)} %vis_u_hbm.1, ...), custom_call_target="tpu_custom_call" | custom-call | tf_op jit(solution)/shard_map/column/pallas_call | solution.py:575
  38.3 1.0 %deliver.1 = (f32[1,2,2048]{2,1,0:T(2,128)}, bf16[1024,512]{1,0:T(8,128)(2,1)}) custom-call(f32[1,2,2048]{2,1,0:T(2,128)S(1)} %get-tuple-element.4.residual, bf16[1024,512]{1,0:T(8,128)(2,1)S(1)} %get-tuple-element.5.update), custom_call_target="tpu_custom_call" | custom-call | tf_op jit(solution)/shard_map/deliver/pallas_call | solution.py:633

commit v3 on v2

--- a/solution.py
+++ b/solution.py
@@ -64,15 +64,19 @@
     return 2 if groups <= M // 16 else 1
 
 
+def layers(n_facet, groups):
+    return n_facet if groups <= M // 16 else 1
+
+
 def far_first(count):
     return sorted(range(1, count), key=lambda j: (-min(j, count - j), j))
 
 
 def kernel(
     sizes,
-    facet_rows,
+    facet_rows_hbm,
     column_offset,
-    subgrid_offsets,
+    subgrid_offsets_hbm,
     counts,
     sky_hbm,
     vis_u_hbm,
@@ -80,7 +84,13 @@
     observed_hbm,
     weights_hbm,
     residual_out,
-    update,
+    t5,
+    t6,
+    zed,
+    partial,
+    wave,
+    facet_rows,
+    subgrid_offsets,
     sky,
     vis_u,
     vis_v,
@@ -91,14 +101,10 @@
     t2,
     du,
     dv,
-    t5,
-    t6,
     lhs,
     model,
     acc,
     spread,
-    zed,
-    partial,
     share,
     s_a,
     x_a,
@@ -110,6 +116,7 @@
     r_d,
     sky_sem,
     side_sem,
+    small_sem,
     send_sem,
     recv_sem,
     d_send,
@@ -120,10 +127,11 @@
     parts = halves(groups)
     wide = 2 * M // parts
     half = wide // 2
+    stages = layers(n_facet, groups)
     rows, columns = sky.shape
     tile = min(256, rows)
     vis = vis_u.shape[1]
-    local_cols = update.shape[1]
+    local_cols = t6.shape[2]
     facet, sub, base = lax.axis_index("facet"), lax.axis_index("sub"), lax.axis_index("base")
     pairs = n_base // 2
     half_group = groups // 2
@@ -152,11 +160,28 @@
         (facet * pairs + q, {"facet": facet, "sub": sub, "base": q * 2 + parity})
         for q in [lax.rem(row_of_base + d, pairs) for d in range(1, pairs)]
     ]
+    steps = [(a, b) for a in range(n_sub) for b in range(pairs)][1:]
+    steps.sort(key=lambda ab: (not (ab[0] and ab[1]), bool(ab[0])))
     levels = [
-        {"facet": facet, "sub": other // pairs, "base": lax.rem(other, pairs) * 2 + parity}
-        for other in [lax.rem(spot + j, plane) for j in far_first(plane)]
+        {
+            "facet": facet,
+            "sub": lax.rem(sub + a, n_sub),
+            "base": lax.rem(row_of_base + b, pairs) * 2 + parity,
+        }
+        for a, b in steps
     ]
 
+    smalls = [
+        pltpu.make_async_copy(source, target, small_sem.at[i])
+        for i, (source, target) in enumerate(
+            (
+                (facet_rows_hbm, facet_rows),
+                (subgrid_offsets_hbm, subgrid_offsets),
+            )
+        )
+    ]
+    for small in smalls:
+        small.start()
     fetches = []
     for i in range(rows // tile):
         here = pl.ds(i * tile, tile)
@@ -270,8 +295,6 @@
             t1[c, a * high : (a + 1) * high, half:] = (sine * -norm).astype(BF16)
 
         phase_product([x[:, lanes] for x in coarse_1], [x[:, lanes] for x in fine_1], put)
-
-    row_start = facet_rows[facet] + base * rows
 
     def make_spec(c):
         for i in range(rows // tile):
@@ -309,7 +332,11 @@
 
             phase_product(coarse, fine, put)
 
-    make_t1(0)
+    for c in range(parts):
+        make_t1(c)
+    for small in smalls:
+        small.wait()
+    row_start = facet_rows[facet] + base * rows
     positions = row_start + lanes_iota(rows)
     own_offset = subgrid_offsets[sub]
     coarse_2 = unit(own_offset + rows_iota(M // step, step), positions, NIMG)
@@ -320,19 +347,18 @@
         t2[a * step : (a + 1) * step, rows:] = s.astype(BF16)
 
     phase_product(coarse_2, fine_2, put_t2)
+
     swaps = []
     for c in range(parts):
         make_spec(c)
-        if c:
-            swaps[c - 1].wait()
-            scatter(1, c - 1, s_a, x_a, r_a)
         contribution(c)
         if not c:
             pl.semaphore_wait(barrier, partners)
         swaps.append(swap(0, c, s_a, x_a))
         swaps[c].start()
-        if c + 1 < parts:
-            make_t1(c + 1)
+        if c:
+            swaps[c - 1].wait()
+            scatter(1, c - 1, s_a, x_a, r_a)
     for side in sides:
         side.wait()
     grid_table(vis_u, du)
@@ -344,14 +370,20 @@
         r_b[c, parity * half_group + pair] = summed(r_a, c)
         gather(2, c, r_b)
 
+    span = M // 2 // stages
+    run = n_sub * 2 * span
+    lane = lanes_iota(run)
+    start = lax.rem(lane // span, 2) * (M // 2) + lax.rem(lane, span)
     for s in range(n_sub):
-        freqs = subgrid_offsets[s] + lanes_iota(M)
+        start = start + jnp.where(lane // (2 * span) == s, subgrid_offsets[s], 0)
+    for k in range(stages):
+        freqs = start + sources[k] * span if stages > 1 else start
         coarse = unit(row_start + rows_iota(rows // high, high), freqs, NIMG)
         fine = unit(rows_iota(high), freqs, NIMG)
 
-        def put_t5(a, c, sine, at=2 * M * s):
-            t5[a * high : (a + 1) * high, at : at + M] = c.astype(BF16)
-            t5[a * high : (a + 1) * high, at + M : at + 2 * M] = sine.astype(BF16)
+        def put_t5(a, c, sine, at=2 * run * k):
+            t5[a * high : (a + 1) * high, at : at + run] = c.astype(BF16)
+            t5[a * high : (a + 1) * high, at + run : at + 2 * run] = sine.astype(BF16)
 
         phase_product(coarse, fine, put_t5)
 
@@ -431,12 +463,12 @@
             )
         acc[:M, :half] = acc[:M, :half] - acc[M:, half:]
         acc[:M, half:] = acc[:M, half:] + acc[M:, :half]
+        split(c, s_c, F32((vis * groups) ** (-0.5)))
+        swaps.append(swap(4, c, s_c, x_c))
+        swaps[c].start()
         if c:
             swaps[c - 1].wait()
             scatter(5, c - 1, s_c, x_c, r_c)
-        split(c, s_c, F32((vis * groups) ** (-0.5)))
-        swaps.append(swap(4, c, s_c, x_c))
-        swaps[c].start()
 
     out_cols = sub * local_cols + lanes_iota(local_cols)
     coarse = unit(column_offset[0] + rows_iota(M // step, step), out_cols, NIMG)
@@ -486,47 +518,93 @@
             device = {"facet": sources[k], "sub": sub, "base": base}
             column_copy(c, k, facet, device, facet).start()
         level_sends(c, facet)
-    for c in range(parts):
+    scale = F32((n_sub * M) ** (-0.5))
+
+    def pass_on(c):
         for k in range(1, n_facet):
             column_copy(c, k, sources[k], sibling, sources[k]).wait_recv()
             level_sends(c, sources[k])
-    for c in range(parts):
-        for f in sources:
+
+    def land(c, k):
+        for f in [sources[k]] if stages > 1 else sources:
             level_done(c, f).wait_recv()
             level_relay(c, f).start()
 
-    scale = F32((n_sub * M) ** (-0.5))
-    for c in range(parts):
-        for f in sources:
+    def build(c, k):
+        for f in [sources[k]] if stages > 1 else sources:
             level_relay(c, f).wait_recv()
-        for s in range(n_sub):
-            top = 2 * M * s
-            for g, r, k, height, width in pieces(groups, wide):
-                which, place = g // half_group, g % half_group
-                block = r_d[c, d_slot(which, place // pairs, s * pairs + place % pairs)]
-                part = min(width, half)
-                low = top + M + r
-                for inner in range(0, width, part):
-                    value = block[:, inner : inner + part]
-                    at = k + inner
-                    zed[c, top + r : top + r + height, at : at + part] = value
-                    if at < half:
-                        zed[c, low : low + height, half + at : half + at + part] = value
-                    else:
-                        zed[c, low : low + height, at - half : at - half + part] = -value
+        for g, r, col, height, width in pieces(groups, wide)[:half_group]:
+            if stages > 1:
+                if g >= pairs:
+                    continue
+                f = sources[k]
+            else:
+                f = g // pairs
+            part = min(width, half)
+            for s in range(n_sub):
+                for which in range(2):
+                    block = r_d[c, d_slot(which, f, s * pairs + g % pairs)]
+                    at = 2 * run * k + (2 * s + which) * span + r
+                    low = slice(at + run, at + run + height)
+                    for inner in range(0, width, part):
+                        value = block[:, inner : inner + part]
+                        to = col + inner
+                        zed[c, at : at + height, to : to + part] = value
+                        if to < half:
+                            zed[c, low, half + to : half + to + part] = value
+                        else:
+                            zed[c, low, to - half : to - half + part] = -value
+
+    def take(c, k):
+        build(c, k)
+        some = slice(2 * run * k, 2 * run * (k + 1))
         for i in range(rows // tile):
             here = slice(i * tile, (i + 1) * tile)
-            wave = jnp.dot(t5[here, :], zed[c], preferred_element_type=F32)
-            share[here, :] = (wave * scale).astype(BF16)
+            term = jnp.dot(t5[here, some], zed[c, some], preferred_element_type=F32)
+            wave[c, here, :] = wave[c, here, :] + term if k else term
+
+    def finish(c):
+        take(c, stages - 1)
+        for i in range(rows // tile):
+            here = slice(i * tile, (i + 1) * tile)
+            share[here, :] = (wave[c, here, :] * scale).astype(BF16)
         for i in range(rows // tile):
             here = slice(i * tile, (i + 1) * tile)
             term = jnp.dot(share[here, :], t6[c], preferred_element_type=F32)
-            if c:
-                term = partial[here, :] + term
+            partial[here, :] = partial[here, :] + term if c else term
+
+    pass_on(0)
+    inner = range(1, stages - 1)
+    if parts == 2 and stages > 1:
+        land(0, 0)
+        pass_on(1)
+        land(1, 0)
+        for k in inner:
+            land(0, k)
+        take(0, 0)
+        take(1, 0)
+        land(0, stages - 1)
+        for k in inner:
+            land(1, k)
+        for k in inner:
+            take(0, k)
+        land(1, stages - 1)
+        for k in inner:
+            take(1, k)
+        finish(0)
+        build(1, stages - 1)
+    else:
+        for c in range(1, parts):
+            pass_on(c)
+        for c in range(parts):
+            for k in range(stages):
+                land(c, k)
+        for c in range(parts):
+            for k in range(stages - 1):
+                take(c, k)
             if c + 1 < parts:
-                partial[here, :] = term
-            else:
-                update[here, :] = term.astype(BF16)
+                finish(c)
+        build(parts - 1, stages - 1)
 
     for c in range(parts):
         for k in range(n_facet):
@@ -536,15 +614,48 @@
                 column_copy(c, k, facet, sibling, facet).wait_send()
 
 
-def deliver(residual, update, residual_out, update_out, sems):
-    copies = [
-        pltpu.make_async_copy(residual, residual_out, sems.at[0]),
-        pltpu.make_async_copy(update, update_out, sems.at[1]),
-    ]
-    for copy in copies:
-        copy.start()
-    for copy in copies:
-        copy.wait()
+def deliver(
+    scale,
+    stages,
+    residual,
+    t5,
+    t6,
+    zed,
+    partial,
+    wave,
+    residual_out,
+    update_out,
+    share,
+    update,
+    sem,
+    sems,
+):
+    first = pltpu.make_async_copy(residual, residual_out, sem)
+    first.start()
+    rows, depth = t5.shape
+    tile = min(256, rows)
+    last = zed.shape[0] - 1
+    some = slice(depth - depth // stages, depth)
+    tiles = [slice(i * tile, (i + 1) * tile) for i in range(rows // tile)]
+    writes = []
+    for start in range(0, len(tiles), 2):
+        for here in tiles[start : start + 2]:
+            total = jnp.dot(t5[here, some], zed[last, some], preferred_element_type=F32)
+            if stages > 1:
+                total = wave[last, here, :] + total
+            share[here, :] = (total * F32(scale)).astype(BF16)
+        for i, here in list(enumerate(tiles))[start : start + 2]:
+            term = jnp.dot(share[here, :], t6[last], preferred_element_type=F32)
+            if last:
+                term = partial[here, :] + term
+            update[here, :] = term.astype(BF16)
+            writes.append(
+                pltpu.make_async_copy(update.at[here, :], update_out.at[here, :], sems.at[i])
+            )
+            writes[i].start()
+    first.wait()
+    for write in writes:
+        write.wait()
 
 
 def shards(
@@ -572,15 +683,25 @@
     hbm = pl.BlockSpec(memory_space=pltpu.HBM)
     block = (parts, groups, height, width)
     half_block = (parts, groups // 2, height, width)
-    residual, update = pl.pallas_call(
+    kept = (
+        pltpu.VMEM((rows, 2 * M * n_sub), BF16),
+        pltpu.VMEM((parts, wide, local_cols), BF16),
+        pltpu.VMEM((parts, 2 * M * n_sub, wide), BF16),
+        pltpu.VMEM((rows, local_cols), F32),
+        pltpu.VMEM((parts, rows, wide), F32),
+    )
+    room = sum(math.prod(k.shape) * jnp.dtype(k.dtype).itemsize for k in kept)
+    results = pl.pallas_call(
         functools.partial(kernel, sizes),
         out_shape=(
             pltpu.VMEM(observed.shape, F32),
-            pltpu.VMEM((rows, local_cols), BF16),
+            *kept,
         ),
-        in_specs=[smem] * 4 + [hbm] * 5,
-        out_specs=(vmem, vmem),
+        in_specs=[hbm, smem, hbm, smem] + [hbm] * 5,
+        out_specs=(vmem,) * 6,
         scratch_shapes=[
+            pltpu.SMEM(facet_rows.shape, jnp.int32),
+            pltpu.SMEM(subgrid_offsets.shape, jnp.int32),
             pltpu.VMEM((rows, columns), BF16),
             pltpu.VMEM(vis_u.shape, jnp.int32),
             pltpu.VMEM(vis_v.shape, jnp.int32),
@@ -591,14 +712,10 @@
             pltpu.VMEM((M, 2 * rows), BF16),
             pltpu.VMEM((2 * M, vis), BF16),
             pltpu.VMEM((2 * M, vis), BF16),
-            pltpu.VMEM((rows, 2 * M * n_sub), BF16),
-            pltpu.VMEM((parts, wide, local_cols), BF16),
             pltpu.VMEM((2, M, 2 * M), BF16),
             pltpu.VMEM((2, vis), F32),
             pltpu.VMEM((2 * M, wide), F32),
             pltpu.VMEM((parts, wide, vis), BF16),
-            pltpu.VMEM((parts, 2 * M * n_sub, wide), BF16),
-            pltpu.VMEM((rows, local_cols), F32),
             pltpu.VMEM((rows, wide), BF16),
             pltpu.VMEM(block, BF16),
             pltpu.VMEM(half_block, BF16),
@@ -610,13 +727,14 @@
             pltpu.VMEM((parts, n_sub * groups, height, width), BF16),
             pltpu.SemaphoreType.DMA((rows // min(256, rows),)),
             pltpu.SemaphoreType.DMA((4,)),
+            pltpu.SemaphoreType.DMA((2,)),
             pltpu.SemaphoreType.DMA((6, parts)),
             pltpu.SemaphoreType.DMA((6, parts)),
             pltpu.SemaphoreType.DMA((3, parts, n_facet)),
             pltpu.SemaphoreType.DMA((3, parts, n_facet)),
         ],
         compiler_params=pltpu.CompilerParams(
-            collective_id=0, has_side_effects=True, vmem_limit_bytes=56 * 1024 * 1024
+            collective_id=0, has_side_effects=True, vmem_limit_bytes=61 * 1024 * 1024 - room
         ),
         name="column",
     )(
@@ -631,19 +749,22 @@
         weights,
     )
     return pl.pallas_call(
-        deliver,
+        functools.partial(deliver, (n_sub * M) ** (-0.5), layers(n_facet, groups)),
         out_shape=(
-            jax.ShapeDtypeStruct(residual.shape, F32),
-            jax.ShapeDtypeStruct(update.shape, BF16),
+            jax.ShapeDtypeStruct(observed.shape, F32),
+            jax.ShapeDtypeStruct((rows, local_cols), BF16),
         ),
-        in_specs=[vmem] * 2,
+        in_specs=[vmem] * 6,
         out_specs=(hbm, hbm),
-        scratch_shapes=[pltpu.SemaphoreType.DMA((2,))],
+        scratch_shapes=[
+            pltpu.VMEM((rows, wide), BF16),
+            pltpu.VMEM((rows, local_cols), BF16),
+            pltpu.SemaphoreType.DMA,
+            pltpu.SemaphoreType.DMA((rows // min(256, rows),)),
+        ],
+        compiler_params=pltpu.CompilerParams(vmem_limit_bytes=8 * 1024 * 1024),
         name="deliver",
-    )(
-        pltpu.with_memory_space_constraint(residual, pltpu.VMEM),
-        pltpu.with_memory_space_constraint(update, pltpu.VMEM),
-    )
+    )(*[pltpu.with_memory_space_constraint(r, pltpu.VMEM) for r in results])
 
 
 def solution(mesh):

time: 39.4 us -> 37.9 us (0.962)
  Pallas kernels: 37.3 us -> 35.8 us
    pallas_call x1, Pallas kernels: 36.3 us -> 34.3 us  [shards(): pl.pallas_call(functools.partial(kernel, sizes), out_shape=(pltpu.VMEM(ob...]
    pallas_call x1, Pallas kernels: 1 us -> 1.49 us  [shards(): pl.pallas_call(functools.partial(deliver, (n_sub * M) ** (-0.5), layers(n...]
where the time goes in v3:
time: 37.9 us; the launch traced here: 37.7 us
  Pallas kernels  35.8 us (94%)
  between operations  1.93 us (5%)
    pallas_call x1, Pallas kernels, shards(): pl.pallas_call(functools.partial(kernel, sizes), out_shape=(pltpu.VMEM(ob...  34.3 us
    pallas_call x1, Pallas kernels, shards(): pl.pallas_call(functools.partial(deliver, (n_sub * M) ** (-0.5), layers(n...  1.49 us

profile of v3, /device:TPU:0, one launch (start us, length us, event | category | flops | bytes accessed | tf_op | source)
XLA Modules:
  0.0 37.7 jit_solution(1945075670876372883)
XLA Ops:
  1.9 34.3 %column.1 = (f32[1,2,2048]{2,1,0:T(2,128)S(1)}, bf16[1024,1024]{1,0:T(8,128)(2,1)S(1)}, bf16[2,256,512]{2,1,0:T(8,128)(2,1)S(1)}, bf16[2,1024,256]{2,1,0:T(8,128...) custom-call(s32[4]{0:T(128)} %facet_rows_hbm.1, s32[1]{0:T(128)S(6)} %copy.11.column_offset, ...), custom_call_target="tpu_custom_call" | custom-call | tf_op jit(solution)/shard_map/column/pallas_call | solution.py:694
  36.2 1.5 %deliver.1 = (f32[1,2,2048]{2,1,0:T(2,128)}, bf16[1024,512]{1,0:T(8,128)(2,1)}) custom-call(f32[1,2,2048]{2,1,0:T(2,128)S(1)} %get-tuple-element.8.residual, bf16[1024,1024]{1,0:T(8,128)(2,1)S(1)} %get-tuple-element.9.t5, bf16[2,256,512]{2,1,0:T(8,128)(2,1)S(1)} %get-tuple-element.10.t6, bf16[2,1024,256]{2,1,0:T(8,128)(2,1)S(1)} %get-tuple-element.11.zed, ...), custom_call_target="tpu_custom_call" | custom-call | tf_op jit(solution)/shard_map/deliver/pallas_call | solution.py:751

commit v4 on v3

--- a/solution.py
+++ b/solution.py
@@ -155,7 +155,7 @@
     mates = [
         (f * pairs + q, {"facet": f, "sub": sub, "base": q * 2 + parity})
         for f in sources[:0:-1]
-        for q in [lax.rem(row_of_base + d, pairs) for d in range(pairs)]
+        for q in [lax.rem(row_of_base + d, pairs) for d in range(pairs)[::-1]]
     ] + [
         (facet * pairs + q, {"facet": facet, "sub": sub, "base": q * 2 + parity})
         for q in [lax.rem(row_of_base + d, pairs) for d in range(1, pairs)]
@@ -281,18 +281,19 @@
             target[c, g] = (acc[r : r + height, k : k + width] * scale).astype(BF16)
 
     high = 128
+    fan = 16
     step = 32
     freq = column_offset[0] + lanes_iota(M)
-    coarse_1 = unit(rows_iota(columns // high, high), freq, NIMG)
-    fine_1 = unit(rows_iota(high), freq, NIMG)
+    coarse_1 = unit(rows_iota(columns // step, step), freq, NIMG)
+    fine_1 = unit(rows_iota(step), freq, NIMG)
     norm = F32(columns ** (-0.5))
 
     def make_t1(c):
         lanes = slice(c * half, (c + 1) * half)
 
         def put(a, cosine, sine):
-            t1[c, a * high : (a + 1) * high, :half] = (cosine * norm).astype(BF16)
-            t1[c, a * high : (a + 1) * high, half:] = (sine * -norm).astype(BF16)
+            t1[c, a * step : (a + 1) * step, :half] = (cosine * norm).astype(BF16)
+            t1[c, a * step : (a + 1) * step, half:] = (sine * -norm).astype(BF16)
 
         phase_product([x[:, lanes] for x in coarse_1], [x[:, lanes] for x in fine_1], put)
 
@@ -316,7 +317,6 @@
             acc[here, :] = jnp.dot(t2[here, :], spec[c], preferred_element_type=F32)
         split(c, s_a, F32((rows * groups) ** (-0.5)))
 
-    fan = 16
 
     def grid_table(position, table):
         width = 512
@@ -339,12 +339,12 @@
     row_start = facet_rows[facet] + base * rows
     positions = row_start + lanes_iota(rows)
     own_offset = subgrid_offsets[sub]
-    coarse_2 = unit(own_offset + rows_iota(M // step, step), positions, NIMG)
-    fine_2 = unit(rows_iota(step), positions, NIMG)
+    coarse_2 = unit(own_offset + rows_iota(M // fan, fan), positions, NIMG)
+    fine_2 = unit(rows_iota(fan), positions, NIMG)
 
     def put_t2(a, c, s):
-        t2[a * step : (a + 1) * step, :rows] = c.astype(BF16)
-        t2[a * step : (a + 1) * step, rows:] = s.astype(BF16)
+        t2[a * fan : (a + 1) * fan, :rows] = c.astype(BF16)
+        t2[a * fan : (a + 1) * fan, rows:] = s.astype(BF16)
 
     phase_product(coarse_2, fine_2, put_t2)
 
@@ -633,7 +633,7 @@
     first = pltpu.make_async_copy(residual, residual_out, sem)
     first.start()
     rows, depth = t5.shape
-    tile = min(256, rows)
+    tile = min(512, rows)
     last = zed.shape[0] - 1
     some = slice(depth - depth // stages, depth)
     tiles = [slice(i * tile, (i + 1) * tile) for i in range(rows // tile)]
@@ -760,7 +760,7 @@
             pltpu.VMEM((rows, wide), BF16),
             pltpu.VMEM((rows, local_cols), BF16),
             pltpu.SemaphoreType.DMA,
-            pltpu.SemaphoreType.DMA((rows // min(256, rows),)),
+            pltpu.SemaphoreType.DMA((rows // min(512, rows),)),
         ],
         compiler_params=pltpu.CompilerParams(vmem_limit_bytes=8 * 1024 * 1024),
         name="deliver",

time: 37.9 us -> 37.8 us (level)
  no operation moved by 1% of the time
where the time goes in v4:
time: 37.8 us; the launch traced here: 37.4 us
  Pallas kernels  35.5 us (94%)
  between operations  1.93 us (5%)
    pallas_call x1, Pallas kernels, shards(): pl.pallas_call(functools.partial(kernel, sizes), out_shape=(pltpu.VMEM(ob...  34 us
    pallas_call x1, Pallas kernels, shards(): pl.pallas_call(functools.partial(deliver, (n_sub * M) ** (-0.5), layers(n...  1.43 us

profile of v4, /device:TPU:0, one launch (start us, length us, event | category | flops | bytes accessed | tf_op | source)
XLA Modules:
  0.0 37.4 jit_solution(1438310345336540677)
XLA Ops:
  1.9 34.0 %column.1 = (f32[1,2,2048]{2,1,0:T(2,128)S(1)}, bf16[1024,1024]{1,0:T(8,128)(2,1)S(1)}, bf16[2,256,512]{2,1,0:T(8,128)(2,1)S(1)}, bf16[2,1024,256]{2,1,0:T(8,128...) custom-call(s32[4]{0:T(128)} %facet_rows_hbm.1, s32[1]{0:T(128)S(6)} %copy.11.column_offset, ...), custom_call_target="tpu_custom_call" | custom-call | tf_op jit(solution)/shard_map/column/pallas_call | solution.py:694
  36.0 1.4 %deliver.1 = (f32[1,2,2048]{2,1,0:T(2,128)}, bf16[1024,512]{1,0:T(8,128)(2,1)}) custom-call(f32[1,2,2048]{2,1,0:T(2,128)S(1)} %get-tuple-element.8.residual, bf16[1024,1024]{1,0:T(8,128)(2,1)S(1)} %get-tuple-element.9.t5, bf16[2,256,512]{2,1,0:T(8,128)(2,1)S(1)} %get-tuple-element.10.t6, bf16[2,1024,256]{2,1,0:T(8,128)(2,1)S(1)} %get-tuple-element.11.zed, ...), custom_call_target="tpu_custom_call" | custom-call | tf_op jit(solution)/shard_map/deliver/pallas_call | solution.py:751

commit v5 on v4

--- a/solution.py
+++ b/solution.py
@@ -444,18 +444,16 @@
         res_im = jnp.where(alive, weight * (observed[0, 1:2, lanes] - model_im * inv), F32(0.0))
         residual_out[0, 0:1, lanes] = res_re
         residual_out[0, 1:2, lanes] = res_im
-
-    across = (((1,), (1,)), ((), ()))
-    swaps = []
-    for c in range(parts):
-        for i in range(vis // chunk):
-            lanes = slice(i * chunk, (i + 1) * chunk)
-            r0 = residual_out[0, 0:1, lanes].astype(BF16)
-            r1 = residual_out[0, 1:2, lanes].astype(BF16)
+        r0, r1 = res_re.astype(BF16), res_im.astype(BF16)
+        for c in range(parts):
             cos_u = du[c * half : (c + 1) * half, lanes]
             sin_u = du[M + c * half : M + (c + 1) * half, lanes]
             spread[c, :half, lanes] = cos_u * r0 - sin_u * r1
             spread[c, half:, lanes] = sin_u * r0 + cos_u * r1
+
+    across = (((1,), (1,)), ((), ()))
+    swaps = []
+    for c in range(parts):
         for i in range(2):
             here = slice(i * M, (i + 1) * M)
             acc[here, :] = lax.dot_general(

time: 37.8 us -> 37.6 us (level)
  no operation moved by 1% of the time
where the time goes in v5:
time: 37.6 us; the launch traced here: 37.3 us
  Pallas kernels  35.4 us (94%)
  between operations  1.93 us (5%)
    pallas_call x1, Pallas kernels, shards(): pl.pallas_call(functools.partial(kernel, sizes), out_shape=(pltpu.VMEM(ob...  34 us
    pallas_call x1, Pallas kernels, shards(): pl.pallas_call(functools.partial(deliver, (n_sub * M) ** (-0.5), layers(n...  1.43 us

profile of v5, /device:TPU:0, one launch (start us, length us, event | category | flops | bytes accessed | tf_op | source)
XLA Modules:
  0.0 37.3 jit_solution(4612287137246166083)
XLA Ops:
  1.9 34.0 %column.1 = (f32[1,2,2048]{2,1,0:T(2,128)S(1)}, bf16[1024,1024]{1,0:T(8,128)(2,1)S(1)}, bf16[2,256,512]{2,1,0:T(8,128)(2,1)S(1)}, bf16[2,1024,256]{2,1,0:T(8,128...) custom-call(s32[4]{0:T(128)} %facet_rows_hbm.1, s32[1]{0:T(128)S(6)} %copy.11.column_offset, ...), custom_call_target="tpu_custom_call" | custom-call | tf_op jit(solution)/shard_map/column/pallas_call | solution.py:692
  35.9 1.4 %deliver.1 = (f32[1,2,2048]{2,1,0:T(2,128)}, bf16[1024,512]{1,0:T(8,128)(2,1)}) custom-call(f32[1,2,2048]{2,1,0:T(2,128)S(1)} %get-tuple-element.8.residual, bf16[1024,1024]{1,0:T(8,128)(2,1)S(1)} %get-tuple-element.9.t5, bf16[2,256,512]{2,1,0:T(8,128)(2,1)S(1)} %get-tuple-element.10.t6, bf16[2,1024,256]{2,1,0:T(8,128)(2,1)S(1)} %get-tuple-element.11.zed, ...), custom_call_target="tpu_custom_call" | custom-call | tf_op jit(solution)/shard_map/deliver/pallas_call | solution.py:749
